TPU v7x, 32 devices: a whole 2x2x4 slice. The times are simulated.
32 devices in a mesh: row: 8 (over z, y), col: 4 (over x, core).
Axes of the slice: x: 2, y: 2, z: 4, core: 2. Of those that a mesh axis runs over, the one named last changes fastest.
Arguments:
- image_in: bfloat16 [2048, 1536], P('row', 'col'), may hold values from -6 to 6
- text_in: bfloat16 [2464, 1536], P('row', 'col'), may hold values from -6 to 6
- condition: bfloat16 [16, 1536], P(None, 'row'), may hold values from -6 to 6
- ranges: int32 [16, 2], P('row'), may hold values from 0 to 192, as said below
- mod_weight: bfloat16 [1, 1536, 2, 6, 1536], P(None, 'row', None, None, 'col'), may hold values from -0.15625 to 0.15625
- qkv_weight: bfloat16 [1, 1536, 2, 3, 1536], P(None, 'row', None, None, 'col'), may hold values from -0.15625 to 0.15625
- out_weight: bfloat16 [1, 1536, 2, 1536], P(None, 'row', None, 'col'), may hold values from -2.5 to 2.5
- up_weight: bfloat16 [1, 1536, 2, 6144], P(None, 'row', None, 'col'), may hold values from -0.15625 to 0.15625
- down_weight: bfloat16 [1, 1536, 2, 6144], P(None, 'row', None, 'col'), may hold values from -0.078125 to 0.078125
- image_cot: bfloat16 [2048, 1536], P('row', 'col'), may hold values from -6 to 6
- text_cot: bfloat16 [2464, 1536], P('row', 'col'), may hold values from -6 to 6
Outputs:
- image_out: float32 [2048, 1536], P('row', 'col')
- text_out: float32 [2464, 1536], P('row', 'col')
- grad_image: float32 [2048, 1536], P('row', 'col')
- grad_text: float32 [2464, 1536], P('row', 'col')
- grad_cond: float32 [16, 1536], P(None, 'row')
- grad_mod: float32 [1, 1536, 2, 6, 1536], P(None, 'row', None, None, 'col')
- grad_qkv: float32 [1, 1536, 2, 3, 1536], P(None, 'row', None, None, 'col')
- grad_out: float32 [1, 1536, 2, 1536], P(None, 'row', None, 'col')
- grad_up: float32 [1, 1536, 2, 6144], P(None, 'row', None, 'col')
- grad_down: float32 [1, 1536, 2, 6144], P(None, 'row', None, 'col')
Inputs may be any that keep to these rules, and one draw needn't show every extreme that they name: `ranges`: each index of row has 2 slots; the first always holds 154 text rows and a multiple of 64 image rows; the second is empty or holds 154 text rows and exactly the image rows the first leaves over, so that index's 256 image rows are full.
All inputs are finite; a program needn't handle non-finite values.
Results may differ from a plain program's by a relative error of at most 0.015.
The roundings to bfloat16 on the way count: a program that leaves them out, or rounds other values in their place, can miss the bound.
Values may be sent and summed in bfloat16 or wider, within the bound.
A program may use at most 320 MiB of HBM per device.

v0:
```python
import math
import jax
import jax.numpy as jnp
from jax import lax
from jax.sharding import PartitionSpec as P

D = 1536
LAYERS = 1
IMG_DEV = 256
HD = 64
TXT_DEV = 308
EPSILON = 1e-06
HIGHEST = lax.Precision.HIGHEST


def slot_table(lengths, image_rows, text_rows):
    ends = jnp.cumsum(lengths, axis=0, dtype=jnp.int32)
    starts = ends - lengths
    slot_ids = jnp.arange(lengths.shape[0], dtype=jnp.int32)
    tables = []
    segments = []
    for column, amount in ((0, image_rows), (1, text_rows)):
        places = jnp.arange(amount, dtype=jnp.int32)[:, None]
        inside = ((places >= starts[None, :, column]) & (places < ends[None, :, column])).astype(
            jnp.int32
        )
        tables.append(inside.astype(jnp.float32))
        filled = jnp.sum(inside, axis=1, dtype=jnp.int32)
        segments.append(
            jnp.sum(inside * slot_ids[None, :], axis=1, dtype=jnp.int32)
            + lengths.shape[0] * (1 - filled)
        )
    return (jnp.concatenate(tables, axis=0), jnp.concatenate(segments, axis=0))


def stream_dot(left, right_image, right_text):
    upper = jnp.dot(left[:IMG_DEV], right_image, preferred_element_type=jnp.float32)
    lower = jnp.dot(left[IMG_DEV:], right_text, preferred_element_type=jnp.float32)
    return jnp.concatenate([upper, lower], axis=0)


def stream_outer(left, right):
    upper = jnp.einsum(
        "nk,nf->kf", left[:IMG_DEV], right[:IMG_DEV], preferred_element_type=jnp.float32
    )
    lower = jnp.einsum(
        "nk,nf->kf", left[IMG_DEV:], right[IMG_DEV:], preferred_element_type=jnp.float32
    )
    return (upper, lower)


def row_mod(slot_ones, mod_mine, layer_index, component):
    upper = jnp.dot(slot_ones[:IMG_DEV], mod_mine[:, layer_index, 0, component], precision=HIGHEST)
    lower = jnp.dot(slot_ones[IMG_DEV:], mod_mine[:, layer_index, 1, component], precision=HIGHEST)
    return jnp.concatenate([upper, lower], axis=0)


def slot_sums(slot_ones, rows):
    upper = jnp.dot(slot_ones[:IMG_DEV].T, rows[:IMG_DEV], precision=HIGHEST)
    lower = jnp.dot(slot_ones[IMG_DEV:].T, rows[IMG_DEV:], precision=HIGHEST)
    return jnp.stack([upper, lower], axis=1)


def feature_sums(first, second):
    return lax.psum((jnp.sum(first, axis=1), jnp.sum(second, axis=1)), "col")


def normalize(hidden):
    totals, squares = feature_sums(hidden, hidden * hidden)
    center = totals / D
    spread = squares / D - center * center
    scaling = lax.rsqrt(spread + EPSILON)
    return ((hidden - center[:, None]) * scaling[:, None], scaling[:, None])


def norm_back(grad_hat, normed, scaling):
    first, second = feature_sums(grad_hat, grad_hat * normed)
    return scaling * (grad_hat - first[:, None] / D - normed * (second[:, None] / D))


def gelu_slope(value):
    coeff = math.sqrt(2.0 / math.pi)
    tangent = jnp.tanh(coeff * (value + 0.044715 * value * value * value))
    return 0.5 * (1.0 + tangent) + 0.5 * value * (1.0 - tangent * tangent) * coeff * (
        1.0 + 3.0 * 0.044715 * value * value
    )


def silu_slope(value):
    sigma = jax.nn.sigmoid(value)
    return sigma * (1.0 + value * (1.0 - sigma))


def gather_features(values):
    return lax.all_gather(values, "col", axis=1, tiled=True)


def gather_grads(values):
    return lax.all_gather(values, "col", axis=1, tiled=True)


def scatter_features(values):
    return lax.psum_scatter(values, "col", scatter_dimension=1, tiled=True)


def scatter_back(values):
    return lax.psum_scatter(values, "col", scatter_dimension=1, tiled=True)


def spread_grads(terms, row_count):
    return lax.psum_scatter(
        terms(jnp.int32(0), row_count * lax.axis_size("row")),
        "row",
        scatter_dimension=0,
        tiled=True,
    )


def fold_rows(left, weight):
    portion = lax.all_gather(weight, "row", axis=0, tiled=True)
    return stream_dot(left, portion[:, 0], portion[:, 1])


def map_rows(left, weight):
    portion = lax.all_gather(weight, "row", axis=0, tiled=True)
    return stream_dot(left, portion[:, 0].T, portion[:, 1].T)


def apply_in(left, weight):
    result = fold_rows(left, weight)
    return result


def apply_out(left, weight):
    result = map_rows(left, weight)
    return result


def mlp_part(operands):
    grad_full, gathered, grad_lifted, activated = operands
    up_image, up_text = stream_outer(gathered, grad_lifted)
    down_image, down_text = stream_outer(grad_full, activated)
    image_part = jnp.concatenate([up_image, down_image], axis=1)
    text_part = jnp.concatenate([up_text, down_text], axis=1)
    return jnp.stack([image_part, text_part], axis=1)


def attention_part(operands):
    grad_full, gathered, grad_projected, mixed = operands
    qkv_image, qkv_text = stream_outer(gathered, grad_projected)
    out_image, out_text = stream_outer(grad_full, mixed)
    image_part = jnp.concatenate([qkv_image, out_image], axis=1)
    text_part = jnp.concatenate([qkv_text, out_text], axis=1)
    return jnp.stack([image_part, text_part], axis=1)


def attend_head(operands, segments, scale):
    queries, key_rows, value_rows = operands
    scores = jnp.dot(queries, key_rows.T, preferred_element_type=jnp.float32) * scale
    allowed = segments[:, None] == segments[None, :]
    scores = jnp.where(allowed, scores, -jnp.inf)
    highest = jnp.max(scores, axis=1, keepdims=True)
    log_total = highest + jnp.log(jnp.sum(jnp.exp(scores - highest), axis=1, keepdims=True))
    weights = jnp.exp(scores - log_total).astype(jnp.bfloat16)
    output = jnp.dot(weights, value_rows, preferred_element_type=jnp.float32).astype(jnp.bfloat16)
    return (output, log_total[:, 0])


def attend_back_head(operands, segments, scale):
    queries, key_rows, value_rows, output, grad_output, log_total = operands
    scores = jnp.dot(queries, key_rows.T, preferred_element_type=jnp.float32) * scale
    allowed = segments[:, None] == segments[None, :]
    scores = jnp.where(allowed, scores, -jnp.inf)
    probs = jnp.exp(scores - log_total[:, None])
    grad_values = jnp.dot(
        probs.astype(jnp.bfloat16).T, grad_output, preferred_element_type=jnp.float32
    )
    grad_probs = jnp.dot(grad_output, value_rows.T, preferred_element_type=jnp.float32)
    inner = jnp.sum(
        grad_output.astype(jnp.float32) * output.astype(jnp.float32), axis=1, keepdims=True
    )
    grad_scores = (probs * (grad_probs - inner) * scale).astype(jnp.bfloat16)
    grad_queries = jnp.dot(grad_scores, key_rows, preferred_element_type=jnp.float32)
    grad_keys = jnp.dot(grad_scores.T, queries, preferred_element_type=jnp.float32)
    return jnp.stack([grad_queries, grad_keys, grad_values], axis=0).astype(jnp.bfloat16)


def per_device(
    image_in,
    text_in,
    condition,
    ranges,
    mod_weight,
    qkv_weight,
    out_weight,
    up_weight,
    down_weight,
    image_cot,
    text_cot,
):
    slot_ones, segments = slot_table(ranges, IMG_DEV, TXT_DEV)
    col_width = image_in.shape[1]
    ff_width = up_weight.shape[3]
    row_count = qkv_weight.shape[1]
    heads_here = col_width // HD
    scale = 1.0 / math.sqrt(HD)
    silu_cond = jax.nn.silu(condition.astype(jnp.float32)).astype(jnp.bfloat16)
    mod_terms = jnp.einsum(
        "sd,ldxkf->slxkf", silu_cond, mod_weight, preferred_element_type=jnp.float32
    )
    mod_mine = lax.psum_scatter(mod_terms, "row", scatter_dimension=0, tiled=True)
    hidden = jnp.concatenate([image_in, text_in], axis=0).astype(jnp.float32)
    layer_index = 0
    qkv_local = qkv_weight[layer_index].reshape(row_count, 2, 3 * col_width)
    whole = (None, None, None, None)
    mods = [row_mod(slot_ones, mod_mine, layer_index, part_no) for part_no in range(6)]
    normed_one, scaling_one = normalize(hidden)
    modulated_one = (normed_one * (1.0 + mods[1]) + mods[0]).astype(jnp.bfloat16)
    gathered_one = gather_features(modulated_one)
    projected = apply_in(gathered_one, qkv_local).astype(jnp.bfloat16)
    heads_form = projected.reshape(-1, 3, heads_here, HD).transpose(1, 2, 0, 3)
    attended, log_totals = lax.map(
        lambda operands: attend_head(operands, segments, scale),
        (heads_form[0], heads_form[1], heads_form[2]),
    )
    mixed = attended.transpose(1, 0, 2).reshape(-1, col_width)
    branch_one = scatter_features(apply_out(mixed, out_weight[layer_index]))
    midway = hidden + mods[2] * branch_one
    normed_two, scaling_two = normalize(midway)
    modulated_two = (normed_two * (1.0 + mods[4]) + mods[3]).astype(jnp.bfloat16)
    gathered_two = gather_features(modulated_two)
    lifted = apply_in(gathered_two, up_weight[layer_index])
    activated = jax.nn.gelu(lifted, approximate=True).astype(jnp.bfloat16)
    branch_two = scatter_features(apply_out(activated, down_weight[layer_index]))
    hidden = midway + mods[5] * branch_two
    saved = [
        (
            whole,
            normed_one,
            scaling_one,
            gathered_one,
            heads_form,
            attended,
            log_totals,
            mixed,
            branch_one,
            normed_two,
            scaling_two,
            gathered_two,
            lifted,
            activated,
            branch_two,
        )
    ]
    image_out = hidden[:IMG_DEV]
    text_out = hidden[IMG_DEV:]
    grad_hidden = jnp.concatenate([image_cot, text_cot], axis=0).astype(jnp.float32)
    grads_qkv = [None] * LAYERS
    grads_out = [None] * LAYERS
    grads_up = [None] * LAYERS
    grads_down = [None] * LAYERS
    grads_slots = [None] * LAYERS
    for layer_index in reversed(range(LAYERS)):
        (
            whole,
            normed_one,
            scaling_one,
            gathered_one,
            heads_form,
            attended,
            log_totals,
            mixed,
            branch_one,
            normed_two,
            scaling_two,
            gathered_two,
            lifted,
            activated,
            branch_two,
        ) = saved[layer_index]
        qkv_local = qkv_weight[layer_index].reshape(row_count, 2, 3 * col_width)
        mods = [row_mod(slot_ones, mod_mine, layer_index, part_no) for part_no in range(6)]
        grad_branch_two = (grad_hidden * mods[5]).astype(jnp.bfloat16)
        gate_two_rows = grad_hidden * branch_two
        grad_full_two = gather_grads(grad_branch_two)
        grad_act = apply_in(grad_full_two, down_weight[layer_index])
        grad_lifted = (grad_act * gelu_slope(lifted)).astype(jnp.bfloat16)
        mlp_operands = (grad_full_two, gathered_two, grad_lifted, activated)
        mlp_grads = spread_grads(lambda offset, amount: mlp_part(mlp_operands), row_count)
        grads_up[layer_index] = mlp_grads[:, :, :ff_width]
        grads_down[layer_index] = mlp_grads[:, :, ff_width:]
        grad_mod_two = scatter_back(apply_out(grad_lifted, up_weight[layer_index]))
        scale_two_rows = grad_mod_two * normed_two
        grad_hidden = grad_hidden + norm_back(
            grad_mod_two * (1.0 + mods[4]), normed_two, scaling_two
        )
        grad_branch_one = (grad_hidden * mods[2]).astype(jnp.bfloat16)
        gate_one_rows = grad_hidden * branch_one
        grad_full_one = gather_grads(grad_branch_one)
        grad_mixed = apply_in(grad_full_one, out_weight[layer_index]).astype(jnp.bfloat16)
        grad_heads = grad_mixed.reshape(-1, heads_here, HD).transpose(1, 0, 2)
        grad_parts = lax.map(
            lambda operands: attend_back_head(operands, segments, scale),
            (heads_form[0], heads_form[1], heads_form[2], attended, grad_heads, log_totals),
        )
        grad_projected = grad_parts.transpose(2, 1, 0, 3).reshape(-1, 3 * col_width)
        attention_operands = (grad_full_one, gathered_one, grad_projected, mixed)
        attention_grads = spread_grads(
            lambda offset, amount: attention_part(attention_operands), row_count
        )
        grads_qkv[layer_index] = attention_grads[:, :, : 3 * col_width].reshape(
            row_count, 2, 3, col_width
        )
        grads_out[layer_index] = attention_grads[:, :, 3 * col_width :]
        grad_mod_one = scatter_back(apply_out(grad_projected, qkv_local))
        scale_one_rows = grad_mod_one * normed_one
        grad_hidden = grad_hidden + norm_back(
            grad_mod_one * (1.0 + mods[1]), normed_one, scaling_one
        )
        rows_list = [
            grad_mod_one,
            scale_one_rows,
            gate_one_rows,
            grad_mod_two,
            scale_two_rows,
            gate_two_rows,
        ]
        grads_slots[layer_index] = jnp.stack(
            [slot_sums(slot_ones, rows) for rows in rows_list], axis=2
        )
    mod_all = lax.all_gather(jnp.stack(grads_slots, axis=1), "row", axis=0, tiled=True)
    grad_mod = jnp.einsum(
        "sd,slxkf->ldxkf", silu_cond.astype(jnp.float32), mod_all, precision=HIGHEST
    )
    cond_part = jnp.einsum(
        "slxkf,ldxkf->sd", mod_all, mod_weight.astype(jnp.float32), precision=HIGHEST
    )
    cond_total = lax.psum(cond_part, "col")
    grad_cond = cond_total * silu_slope(condition.astype(jnp.float32))
    grad_image = grad_hidden[:IMG_DEV]
    grad_text = grad_hidden[IMG_DEV:]
    return (
        image_out,
        text_out,
        grad_image,
        grad_text,
        grad_cond,
        grad_mod,
        jnp.stack(grads_qkv),
        jnp.stack(grads_out),
        jnp.stack(grads_up),
        jnp.stack(grads_down),
    )


def solution(mesh):
    return jax.shard_map(
        per_device,
        mesh=mesh,
        in_specs=(
            P("row", "col"),
            P("row", "col"),
            P(None, "row"),
            P("row", None),
            P(None, "row", None, None, "col"),
            P(None, "row", None, None, "col"),
            P(None, "row", None, "col"),
            P(None, "row", None, "col"),
            P(None, "row", None, "col"),
            P("row", "col"),
            P("row", "col"),
        ),
        out_specs=(
            P("row", "col"),
            P("row", "col"),
            P("row", "col"),
            P("row", "col"),
            P(None, "row"),
            P(None, "row", None, None, "col"),
            P(None, "row", None, None, "col"),
            P(None, "row", None, "col"),
            P(None, "row", None, "col"),
            P(None, "row", None, "col"),
        ),
        check_vma=False,
    )
```

profile of v0, /device:TPU:0, one launch (start us, length us, event | category | flops | bytes accessed | tf_op | source)
XLA Modules:
  0.0 2627.9 jit_solution(4866509215842069157)
XLA Ops:
  15.9 8.5 all-reduce.6
  24.7 61.2 %all-reduce.11.cloned.1.call-done = f32[16,1,2,6,384]{4,0,3,2,1:T(8,128)} async-done(((f32[16,1,2,6,384]{4,0,3,2,1:T(8,128)}), f32[16,1,2,6,384]{4,0,3,2,1:T(8,128)}) %all-reduce.11.cloned.1.call-update) | async-done | bytes 294928
  95.3 100.8 %all-gather.15.cloned.1.call-done = bf16[1536,2,1152]{2,0,1:T(8,128)(2,1)} async-done(((bf16[192,2,1152]{2,0,1:T(8,128)(2,1)}), bf16[1536,2,1152]{2,0,1:T(8,128)(2,1)}) %all-gather.15.cloned.1.call-update) | async-done | bytes 7077904 | tf_op jit(solution)/shard_map/all_gather | solution.py:120
  196.0 6.6 slice_bitcast_fusion.13
  202.6 5.8 copy.120
  208.4 5.8 copy.119
  229.1 16.3 while.22
  249.0 22.4 all-gather.23.cloned.1.call-done
  297.1 17.9 reduce-scatter.6.cloned.1.call-done
  316.8 5.9 all-reduce.5
  325.0 12.6 all-gather.19.cloned.1.call-done
  337.6 140.0 %all-gather.27.cloned.1.call-done = bf16[1,1536,2,1536]{3,1,2,0:T(8,128)(2,1)} async-done(((bf16[1,192,2,1536]{3,1,2,0:T(8,128)(2,1)}), bf16[1,1536,2,1536]{3,1,2,0:T(8,128)(2,1)}) %all-gather.27.cloned.1.call-update) | async-done | bytes 9437200 | tf_op jit(solution)/shard_map/all_gather | solution.py:125
  488.2 127.7 %all-gather.25.cloned.1.call-done = bf16[1,1536,2,1536]{3,1,2,0:T(8,128)(2,1)} async-done(((bf16[1,192,2,1536]{3,1,2,0:T(8,128)(2,1)}), bf16[1,1536,2,1536]{3,1,2,0:T(8,128)(2,1)}) %all-gather.25.cloned.1.call-update) | async-done | bytes 9437200 | tf_op jit(solution)/shard_map/all_gather | solution.py:120
  615.9 20.9 all-gather.17.cloned.1.call-done
  665.1 29.2 %reduce-scatter.10.cloned.1.call-done = f32[564,384]{1,0:T(8,128)} async-done(((f32[564,1536]{1,0:T(8,128)}), f32[564,384]{1,0:T(8,128)}) %reduce-scatter.10.cloned.1.call-update) | async-done | bytes 866320 | tf_op jit(solution)/shard_map/reduce_scatter | solution.py:107
  696.2 6.4 all-reduce.4
  703.3 34.0 %reduce-scatter.8.cloned.1.call-done = f32[564,384]{1,0:T(8,128)} async-done(((f32[564,1536]{1,0:T(8,128)}), f32[564,384]{1,0:T(8,128)}) %reduce-scatter.8.cloned.1.call-update) | async-done | bytes 866320 | tf_op jit(solution)/shard_map/reduce_scatter | solution.py:103
  743.6 9.1 reduce-scatter.12.cloned.1.call-start
  769.1 64.8 %while.23 = (s32[]{:T(128)}, bf16[6,3,564,64]{2,3,0,1:T(8,128)(2,1)}, s32[564]{0:T(1024)}, bf16[6,564,64]{2,1,0:T(8,128)(2,1)}, bf16[6,564,64]{2,1,0:T(8,128)(2,...) while((s32[]{:T(128)}, ...), condition=%wide.region_27.28_spmd, body=%wide.region_25.27_spmd.sunk | while | flops 207346144 | bytes 8018613 | solution.py:302
  859.0 8.2 maximum_bitcast_fusion.4
  867.3 7.8 maximum_bitcast_fusion.3
  875.0 14.7 pad_maximum_fusion.1
  889.7 28.5 %copy.139 = f32[1536,2,1536]{2,1,0:T(2,128)} copy(f32[1536,2,1536]{0,2,1:T(8,128)} %pad_maximum_fusion.1) | data formatting | bytes 37748736 | tf_op jit(solution)/shard_map/stack | solution.py:154
  937.3 7.8 maximum_bitcast_fusion.2
  945.1 11.3 maximum_bitcast_fusion.1
  956.4 21.2 pad_maximum_fusion
  977.5 55.5 %copy.141 = f32[1536,2,3072]{2,1,0:T(2,128)} copy(f32[1536,2,3072]{0,2,1:T(8,128)} %pad_maximum_fusion) | data formatting | bytes 75497472 | tf_op jit(solution)/shard_map/stack | solution.py:145
  1054.0 33.8 %all-gather.3 = f32[16,2,6,384]{3,1,2,0:T(2,128)S(1)} all-gather(f32[2,2,6,384]{3,1,2,0:T(2,128)S(1)} %copy.135), channel_id=5, replica_groups=mesh['row'=8,'col'=4] {'row'}, dimensions={0}, use_global_device_ids=true | all-gather | bytes 331776 | tf_op jit(solution)/shard_map/all_gather | solution.py:331
  1090.0 11.9 all-reduce.3
  1112.1 376.4 %all-reduce.13.cloned.1.call-done = f32[1536,2,1536]{2,1,0:T(2,128)} async-done(((f32[1536,2,1536]{2,1,0:T(2,128)}), f32[1536,2,1536]{2,1,0:T(2,128)}) %all-reduce.13.cloned.1.call-update) | async-done | bytes 18874384
  1494.4 1118.8 %all-reduce.15.cloned.1.call-done = f32[1536,2,3072]{2,1,0:T(2,128)} async-done(((f32[1536,2,3072]{2,1,0:T(2,128)}), f32[1536,2,3072]{2,1,0:T(2,128)}) %all-reduce.15.cloned.1.call-update) | async-done | bytes 37748752
  2613.2 7.8 dynamic-slice_bitcast_fusion
  (387 shorter events, 292.2 us)
Async XLA Ops:
  7.2 78.7 %all-reduce.11.cloned.1.call-start = ((), (), s32[]{:S(2)}) async-start(), calls=%async_computation.16 | async-start | bytes 589824
  10.5 185.5 %all-gather.15.cloned.1.call-start = ((), (), s32[]{:S(2)}) async-start(), calls=%async_computation.5 | async-start | bytes 7962624 | tf_op jit(solution)/shard_map/all_gather | solution.py:120
  14.3 202.7 %all-gather.13.cloned.1.call-start = ((), (), s32[]{:S(2)}) async-start(), calls=%async_computation.4 | async-start | bytes 2181120 | tf_op jit(solution)/shard_map/all_gather | solution.py:95
  24.6 264.2 %copy-start.45 = (s32[2]{0:T(128)}, s32[2]{0:T(128)S(1)}, u32[]{:S(2)}) copy-start(s32[2]{0:T(128)S(1)} %get-tuple-element.240) | copy-start | bytes 28
  24.7 264.2 %copy-start.47 = (s32[2]{0:T(128)}, s32[2]{0:T(128)S(1)}, u32[]{:S(2)}) copy-start(s32[2]{0:T(128)S(1)} %get-tuple-element.315) | copy-start | bytes 28
  24.7 270.1 %copy-start.49 = (s32[2]{0:T(128)}, s32[2]{0:T(128)S(1)}, u32[]{:S(2)}) copy-start(s32[2]{0:T(128)S(1)} %get-tuple-element.241) | copy-start | bytes 28
  24.7 270.1 %copy-start.51 = (s32[2]{0:T(128)}, s32[2]{0:T(128)S(1)}, u32[]{:S(2)}) copy-start(s32[2]{0:T(128)S(1)} %get-tuple-element.314) | copy-start | bytes 28
  24.7 68.8 %copy-start.54 = (f32[564]{0:T(1024)}, f32[564]{0:T(1024)S(1)}, u32[]{:S(2)}) copy-start(f32[564]{0:T(1024)S(1)} %get-tuple-element.312) | copy-start | bytes 6772
  24.7 68.8 %copy-start.56 = (f32[564]{0:T(1024)}, f32[564]{0:T(1024)S(1)}, u32[]{:S(2)}) copy-start(f32[564]{0:T(1024)S(1)} %get-tuple-element.313) | copy-start | bytes 6772
  93.6 177.9 %all-gather.23.cloned.1.call-start = ((), (), s32[]{:S(2)}) async-start(), calls=%async_computation.13 | async-start | bytes 2654208 | tf_op jit(solution)/shard_map/all_gather | solution.py:125
  94.4 220.6 %reduce-scatter.6.cloned.1.call-start = ((), (), s32[]{:S(2)}) async-start(), calls=%async_computation.6 | async-start | bytes 4362240 | tf_op jit(solution)/shard_map/reduce_scatter | solution.py:103
  245.4 28.9 %copy-start.17 = (bf16[6,564,64]{2,1,0:T(8,128)(2,1)}, bf16[6,564,64]{2,1,0:T(8,128)(2,1)S(1)}, u32[]{:S(2)}) copy-start(bf16[6,564,64]{2,1,0:T(8,128)(2,1)S(1)} %get-tuple-element.510) | copy-start | bytes 1299460
  245.4 28.9 %copy-start.28 = (bf16[6,564,64]{2,1,0:T(8,128)(2,1)}, bf16[6,564,64]{2,1,0:T(8,128)(2,1)S(1)}, u32[]{:S(2)}) copy-start(bf16[6,564,64]{2,1,0:T(8,128)(2,1)S(1)} %get-tuple-element.518) | copy-start | bytes 1299460
  276.4 61.2 %all-gather.19.cloned.1.call-start = ((), (), s32[]{:S(2)}) async-start(), calls=%async_computation.9 | async-start | bytes 2181120 | tf_op jit(solution)/shard_map/all_gather | solution.py:99
  281.5 196.2 %all-gather.27.cloned.1.call-start = ((), (), s32[]{:S(2)}) async-start(), calls=%async_computation.15 | async-start | bytes 10616832 | tf_op jit(solution)/shard_map/all_gather | solution.py:125
  282.7 333.2 %all-gather.25.cloned.1.call-start = ((), (), s32[]{:S(2)}) async-start(), calls=%async_computation.14 | async-start | bytes 10616832 | tf_op jit(solution)/shard_map/all_gather | solution.py:120
  285.5 351.3 %all-gather.17.cloned.1.call-start = ((), (), s32[]{:S(2)}) async-start(), calls=%async_computation.7 | async-start | bytes 2181120 | tf_op jit(solution)/shard_map/all_gather | solution.py:95
  288.9 33.8 %copy-start.14 = (f32[256,384]{1,0:T(8,128)}, f32[256,384]{1,0:T(8,128)S(1)}, u32[]{:S(2)}) copy-start(f32[256,384]{1,0:T(8,128)S(1)} %fusion.196) | copy-start | bytes 1179652
  294.8 30.1 %copy-start.7 = (f32[308,384]{1,0:T(8,128)}, f32[308,384]{1,0:T(8,128)S(1)}, u32[]{:S(2)}) copy-start(f32[308,384]{1,0:T(8,128)S(1)} %fusion.163) | copy-start | bytes 1419268
  325.0 369.3 %reduce-scatter.10.cloned.1.call-start = ((), (), s32[]{:S(2)}) async-start(), calls=%async_computation.10 | async-start | bytes 4362240 | tf_op jit(solution)/shard_map/reduce_scatter | solution.py:107
  654.2 83.1 %reduce-scatter.8.cloned.1.call-start = ((), (), s32[]{:S(2)}) async-start(), calls=%async_computation.8 | async-start | bytes 4362240 | tf_op jit(solution)/shard_map/reduce_scatter | solution.py:103
  665.1 99.2 %all-gather.21.cloned.1.call-start = ((), (), s32[]{:S(2)}) async-start(), calls=%async_computation.11 | async-start | bytes 2181120 | tf_op jit(solution)/shard_map/all_gather | solution.py:99
  694.3 43.1 %copy-start.4 = (f32[564,384]{1,0:T(8,128)S(1)}, f32[564,384]{1,0:T(8,128)}, u32[]{:S(2)}) copy-start(f32[564,384]{1,0:T(8,128)} %reduce-scatter.10.cloned.1.call-done) | copy-start | bytes 2598916
  743.6 304.8 %reduce-scatter.12.cloned.1.call-start = ((), (), s32[]{:S(2)}) async-start(), calls=%async_computation.12 | async-start | bytes 4362240 | tf_op jit(solution)/shard_map/reduce_scatter | solution.py:107
  845.6 642.9 %all-reduce.13.cloned.1.call-start = ((), (), s32[]{:S(2)}) async-start(), calls=%async_computation.17 | async-start | bytes 37748736
  918.3 1694.9 %all-reduce.15.cloned.1.call-start = ((), (), s32[]{:S(2)}) async-start(), calls=%async_computation.18 | async-start | bytes 75497472
  1035.8 15.3 copy-start.9
  1035.8 15.3 copy-start.16
  1035.8 15.4 copy-start.55
  1035.8 15.4 copy-start.57
  1053.1 48.8 %copy-start.3 = (f32[564,384]{1,0:T(8,128)S(1)}, f32[564,384]{1,0:T(8,128)}, u32[]{:S(2)}) copy-start(f32[564,384]{1,0:T(8,128)} %copy-done.2) | copy-start | bytes 2598916
  1053.1 48.8 %copy-start.6 = (f32[564,384]{1,0:T(8,128)S(1)}, f32[564,384]{1,0:T(8,128)}, u32[]{:S(2)}) copy-start(f32[564,384]{1,0:T(8,128)} %reduce-scatter.12.cloned.1.call-done) | copy-start | bytes 2598916
  (51 other events, 202.1 us)
Sparse Core Ops, SparseCore 0:
  11.9 73.9 all-reduce.10
  88.7 107.3 all-gather.14
  198.2 18.7 all-gather.12
  219.6 51.8 all-gather.22
  276.5 38.4 reduce-scatter.5
  317.0 20.5 all-gather.18
  340.4 137.2 all-gather.26
  480.4 135.4 all-gather.24
  618.0 18.7 all-gather.16
  654.3 39.8 reduce-scatter.9
  697.4 39.8 reduce-scatter.7
  743.7 20.5 all-gather.20
  845.7 39.8 reduce-scatter.11
  918.4 570.0 all-reduce.12
  1492.6 1120.5 all-reduce.14
where the time goes:
time: 2640 us; the launch traced here: 2630 us
  waiting for transfers between devices  2070 us (78%)
  local copies, waits for them, and re-layouts  178 us (7%)
  matrix products  171 us (6%)
  other arithmetic  116 us (4%)
  blocking collectives  66.6 us (3%)
    unnamed x18, waiting for transfers between devices  1560 us
    all_gather x2, waiting for transfers between devices, fold_rows(): portion = lax.all_gather(weight, 'row', axis=0, tiled=True)  228 us
    all_gather x2, waiting for transfers between devices, map_rows(): portion = lax.all_gather(weight, 'row', axis=0, tiled=True)  162 us
    another operation x1, local copies, waits for them, and re-layouts, mlp_part(): return jnp.stack([image_part, text_part], axis=1)  55.5 us
  transfers between devices with their start and end apart: 15, of which 14 were waited for; matrix products, arithmetic and copies ran while one was open for 13% of the time, Pallas kernels for 0%

commit v1 on v0

--- a/solution.py
+++ b/solution.py
@@ -11,6 +11,27 @@
 TXT_DEV = 308
 EPSILON = 1e-06
 HIGHEST = lax.Precision.HIGHEST
+
+
+def laid_out(blocks, dim):
+    dims = list(blocks.shape[1:])
+    dims[dim] *= blocks.shape[0]
+    return jnp.moveaxis(blocks, 0, dim).reshape(dims)
+
+
+def collected_by_bits(x, axis):
+    peers, index = (lax.axis_size(axis), lax.axis_index(axis))
+    tiles, bit = (x[None], 1)
+    while bit < peers:
+        other = lax.ppermute(tiles, axis, [(i, i ^ bit) for i in range(peers)])
+        low = index & bit == 0
+        tiles = jnp.concatenate([jnp.where(low, tiles, other), jnp.where(low, other, tiles)])
+        bit *= 2
+    return tiles
+
+
+def gather_by_bits(array, axis, dim):
+    return laid_out(collected_by_bits(array, axis), dim)
 
 
 def slot_table(lengths, image_rows, text_rows):
@@ -122,7 +143,7 @@
 
 
 def map_rows(left, weight):
-    portion = lax.all_gather(weight, "row", axis=0, tiled=True)
+    portion = gather_by_bits(weight, "row", 0)
     return stream_dot(left, portion[:, 0].T, portion[:, 1].T)
 
 

time: 2640 us -> 3260 us (1.23)
  waiting for transfers between devices: 2070 us -> 2500 us
  other arithmetic: 116 us -> 247 us
  local copies, waits for them, and re-layouts: 178 us -> 222 us
    ppermute x0 -> x12, waiting for transfers between devices: none -> 772 us  [collected_by_bits(): other = lax.ppermute(tiles, axis, [(i, i ^ bit) for i in range(peers)])]
    all_gather x2 -> x0, waiting for transfers between devices: 162 us -> none  [map_rows(): portion = lax.all_gather(weight, 'row', axis=0, tiled=True)]
    concatenate x0 -> x12, other arithmetic: none -> 73.1 us  [collected_by_bits(): jnp.concatenate([jnp.where(low, tiles, other), jnp.where(low, other, tile...]
    select_n x0 -> x11, other arithmetic: none -> 57.6 us  [collected_by_bits(): jnp.where(low, tiles, other)]
    reduce_scatter x2, waiting for transfers between devices: 51.9 us -> 0.01 us  [scatter_features(): return lax.psum_scatter(values, 'col', scatter_dimension=1, tiled=True)]
    all_gather x2 -> x4, waiting for transfers between devices: 228 us -> 177 us  [fold_rows(): portion = lax.all_gather(weight, 'row', axis=0, tiled=True)]
  transfers between devices with their start and end apart: 15 -> 27, of which waited for: 14 -> 17; matrix products, arithmetic and copies ran while one was open for 13% -> 15% of each run, Pallas kernels for 0% -> 0%
where the time goes in v1:
time: 3260 us; the launch traced here: 3240 us
  waiting for transfers between devices  2500 us (77%)
  other arithmetic  247 us (8%)
  local copies, waits for them, and re-layouts  222 us (7%)
  matrix products  168 us (5%)
  blocking collectives  64 us (2%)
    unnamed x18, waiting for transfers between devices  1550 us
    ppermute x12, waiting for transfers between devices, collected_by_bits(): other = lax.ppermute(tiles, axis, [(i, i ^ bit) for i in range(peers)])  772 us
    all_gather x4, waiting for transfers between devices, fold_rows(): portion = lax.all_gather(weight, 'row', axis=0, tiled=True)  177 us
    concatenate x12, other arithmetic, collected_by_bits(): jnp.concatenate([jnp.where(low, tiles, other), jnp.where(low, other, tile...  73.1 us
  transfers between devices with their start and end apart: 27, of which 17 were waited for; matrix products, arithmetic and copies ran while one was open for 15% of the time, Pallas kernels for 0%

profile of v1, /device:TPU:0, one launch (start us, length us, event | category | flops | bytes accessed | tf_op | source)
XLA Modules:
  0.0 3242.0 jit_solution(10906370512133535611)
XLA Ops:
  52.8 54.2 %all-reduce.11.cloned.1.call-done = f32[16,1,2,6,384]{4,0,3,2,1:T(8,128)} async-done(((f32[16,1,2,6,384]{4,0,3,2,1:T(8,128)}), f32[16,1,2,6,384]{4,0,3,2,1:T(8,128)}) %all-reduce.11.cloned.1.call-update) | async-done | bytes 294928
  123.6 94.0 %all-gather.15.cloned.1.call-done = bf16[1536,2,1152]{2,0,1:T(8,128)(2,1)} async-done(((bf16[192,2,1152]{2,0,1:T(8,128)(2,1)}), bf16[1536,2,1152]{2,0,1:T(8,128)(2,1)}) %all-gather.15.cloned.1.call-update) | async-done | bytes 7077904 | tf_op jit(solution)/shard_map/all_gather | solution.py:141
  250.7 23.8 while.22
  292.8 25.7 collective-permute-done.6
  324.8 18.3 collective-permute-done.3
  349.4 66.0 %collective-permute-done.7 = bf16[2,192,2,1536]{3,2,1,0:T(2,128)(2,1)S(1)} collective-permute-done((bf16[2,192,2,1536]{3,2,1,0:T(2,128)(2,1)S(1)}, bf16[2,192,2,1536]{3,2,1,0:T(2,128)(2,1)S(1)}, u32[]{:S(2)}, u32[]{:S(2)}) %collective-permute-start.7) | collective-permute-done | bytes 2359328 | tf_op jit(solution)/shard_map/ppermute | solution.py:26
  415.4 110.3 %collective-permute-done.4 = bf16[2,192,2,1536]{3,2,1,0:T(2,128)(2,1)S(1)} collective-permute-done((bf16[2,192,2,1536]{3,2,1,0:T(2,128)(2,1)S(1)}, bf16[2,192,2,1536]{3,2,1,0:T(2,128)(2,1)S(1)}, u32[]{:S(2)}, u32[]{:S(2)}) %collective-permute-start.4) | collective-permute-done | bytes 2359328 | tf_op jit(solution)/shard_map/ppermute | solution.py:26
  525.7 13.3 broadcast_select_fusion.5
  539.0 10.6 pad_maximum_fusion.6
  563.3 10.9 pad_maximum_fusion.5
  575.0 387.9 %collective-permute-done.8 = bf16[4,192,2,1536]{3,2,1,0:T(2,128)(2,1)} collective-permute-done((bf16[4,192,2,1536]{3,2,1,0:T(2,128)(2,1)}, bf16[4,192,2,1536]{3,2,1,0:T(2,128)(2,1)}, u32[]{:S(2)}, u32[]{:S(2)}) %collective-permute-start.8) | collective-permute-done | bytes 4718624 | tf_op jit(solution)/shard_map/ppermute | solution.py:26
  962.8 13.0 broadcast_select_fusion.1
  986.1 14.9 pad_maximum_fusion.3
  1001.0 9.3 copy.200
  1037.8 23.9 collective-permute-done.5
  1061.6 12.3 broadcast_select_fusion.3
  1073.9 13.6 pad_maximum_fusion.2
  1087.5 9.2 copy.198
  1110.2 18.1 collective-permute-done.9
  1134.6 46.8 %collective-permute-done.10 = bf16[2,192,2,1152]{3,1,2,0:T(8,128)(2,1)} collective-permute-done((bf16[2,192,2,1152]{3,1,2,0:T(8,128)(2,1)S(1)}, bf16[2,192,2,1152]{3,1,2,0:T(8,128)(2,1)}, u32[]{:S(2)}, u32[]{:S(2)}) %collective-permute-start.10) | collective-permute-done | bytes 1769504 | tf_op jit(solution)/shard_map/ppermute | solution.py:26
  1206.6 83.0 %all-gather.27.cloned.1.call-done = bf16[1,1536,2,384]{3,1,2,0:T(8,128)(2,1)} async-done(((bf16[1,192,2,384]{3,1,2,0:T(8,128)(2,1)}), bf16[1,1536,2,384]{3,1,2,0:T(8,128)(2,1)}) %all-gather.27.cloned.1.call-update) | async-done | bytes 2359312 | tf_op jit(solution)/shard_map/all_gather | solution.py:141
  1297.9 59.3 %collective-permute-done.11 = bf16[4,192,2,1152]{3,1,2,0:T(8,128)(2,1)} collective-permute-done((bf16[4,192,2,1152]{3,1,2,0:T(8,128)(2,1)}, bf16[4,192,2,1152]{3,1,2,0:T(8,128)(2,1)}, u32[]{:S(2)}, u32[]{:S(2)}) %collective-permute-start.11) | collective-permute-done | bytes 3538976 | tf_op jit(solution)/shard_map/ppermute | solution.py:26
  1380.2 69.1 %while.23 = (s32[]{:T(128)}, bf16[6,3,564,64]{2,3,0,1:T(8,128)(2,1)}, s32[564]{0:T(1024)S(1)}, bf16[6,564,64]{2,1,0:T(8,128)(2,1)}, bf16[6,564,64]{2,1,0:T(8,128...) while((s32[]{:T(128)}, ...), condition=%wide.region_27.28_spmd, body=%wide.region_25.27_spmd.sunk | while | flops 207346144 | bytes 8020453 | solution.py:323
  1490.8 14.6 pad_maximum_fusion.1
  1505.4 28.3 copy.216
  1560.1 11.3 maximum_bitcast_fusion.1
  1571.4 21.2 pad_maximum_fusion
  1592.6 55.9 %copy.218 = f32[1536,2,3072]{2,1,0:T(2,128)} copy(f32[1536,2,3072]{0,2,1:T(8,128)} %pad_maximum_fusion) | data formatting | bytes 75497472 | tf_op jit(solution)/shard_map/stack | solution.py:166
  1669.4 33.0 %all-gather.3 = f32[16,2,6,384]{3,1,2,0:T(2,128)S(1)} all-gather(f32[2,2,6,384]{3,1,2,0:T(2,128)S(1)} %copy.212), channel_id=5, replica_groups=mesh['row'=8,'col'=4] {'row'}, dimensions={0}, use_global_device_ids=true | all-gather | bytes 331776 | tf_op jit(solution)/shard_map/all_gather | solution.py:352
  1704.6 11.9 all-reduce.3
  1726.7 375.9 %all-reduce.13.cloned.1.call-done = f32[1536,2,1536]{2,1,0:T(2,128)} async-done(((f32[1536,2,1536]{2,1,0:T(2,128)}), f32[1536,2,1536]{2,1,0:T(2,128)}) %all-reduce.13.cloned.1.call-update) | async-done | bytes 18874384
  2108.4 1118.8 %all-reduce.15.cloned.1.call-done = f32[1536,2,3072]{2,1,0:T(2,128)} async-done(((f32[1536,2,3072]{2,1,0:T(2,128)}), f32[1536,2,3072]{2,1,0:T(2,128)}) %all-reduce.15.cloned.1.call-update) | async-done | bytes 37748752
  (472 shorter events, 459.0 us)
Async XLA Ops:
  7.2 99.7 %all-reduce.11.cloned.1.call-start = ((), (), s32[]{:S(2)}) async-start(), calls=%async_computation.16 | async-start | bytes 589824
  10.5 207.2 %all-gather.15.cloned.1.call-start = ((), (), s32[]{:S(2)}) async-start(), calls=%async_computation.5 | async-start | bytes 7962624 | tf_op jit(solution)/shard_map/all_gather | solution.py:141
  14.1 224.4 %all-gather.13.cloned.1.call-start = ((), (), s32[]{:S(2)}) async-start(), calls=%async_computation.4 | async-start | bytes 2181120 | tf_op jit(solution)/shard_map/all_gather | solution.py:116
  14.2 11.4 collective-permute-start
  17.5 537.6 %copy-start.57 = (s32[2]{0:T(128)}, s32[2]{0:T(128)S(1)}, u32[]{:S(2)}) copy-start(s32[2]{0:T(128)S(1)} %get-tuple-element.292) | copy-start | bytes 28
  17.5 537.6 %copy-start.59 = (s32[2]{0:T(128)}, s32[2]{0:T(128)S(1)}, u32[]{:S(2)}) copy-start(s32[2]{0:T(128)S(1)} %get-tuple-element.393) | copy-start | bytes 28
  17.5 543.5 %copy-start.61 = (s32[2]{0:T(128)}, s32[2]{0:T(128)S(1)}, u32[]{:S(2)}) copy-start(s32[2]{0:T(128)S(1)} %get-tuple-element.293) | copy-start | bytes 28
  17.6 543.5 %copy-start.63 = (s32[2]{0:T(128)}, s32[2]{0:T(128)S(1)}, u32[]{:S(2)}) copy-start(s32[2]{0:T(128)S(1)} %get-tuple-element.392) | copy-start | bytes 28
  28.5 15.8 collective-permute-start.1
  49.4 65.6 %collective-permute-start.2 = (bf16[4,192,2,384]{3,2,1,0:T(2,128)(2,1)}, bf16[4,192,2,384]{3,2,1,0:T(2,128)(2,1)}, u32[]{:S(2)}, u32[]{:S(2)}) collective-permute-start(bf16[4,192,2,384]{3,2,1,0:T(2,128)(2,1)} %pad_maximum_fusion.17), channel_id=1, source_target_pairs={{0,16},{4,20},{8,24},{12,28},{16,0},{20,4},{24,8},{28,12},{1,17},{... | collective-permute-start | bytes 3538952 | tf_op jit(solution)/shard_map/ppermute | solution.py:26
  114.5 861.3 %reduce-scatter.6.cloned.1.call-start = ((), (), s32[]{:S(2)}) async-start(), calls=%async_computation.6 | async-start | bytes 4362240 | tf_op jit(solution)/shard_map/reduce_scatter | solution.py:124
  281.8 728.5 %all-gather.19.cloned.1.call-start = ((), (), s32[]{:S(2)}) async-start(), calls=%async_computation.9 | async-start | bytes 2181120 | tf_op jit(solution)/shard_map/all_gather | solution.py:120
  286.5 723.7 %all-gather.25.cloned.1.call-start = ((), (), s32[]{:S(2)}) async-start(), calls=%async_computation.14 | async-start | bytes 10616832 | tf_op jit(solution)/shard_map/all_gather | solution.py:141
  289.5 731.3 %all-gather.23.cloned.1.call-start = ((), (), s32[]{:S(2)}) async-start(), calls=%async_computation.13 | async-start | bytes 10616832 | tf_op jit(solution)/shard_map/all_gather | solution.py:141
  289.5 29.0 collective-permute-start.6
  291.0 52.1 %collective-permute-start.3 = (bf16[1,192,2,1536]{3,2,1,0:T(2,128)(2,1)}, bf16[1,192,2,1536]{3,2,1,0:T(2,128)(2,1)}, u32[]{:S(2)}, u32[]{:S(2)}) collective-permute-start(bf16[1,192,2,1536]{3,2,1,0:T(2,128)(2,1)} %param.23), channel_id=1, source_target_pairs={{0,4},{4,0},{8,12},{12,8},{16,20},{20,16},{24,28},{28,24},{1,5},{5... | collective-permute-start | bytes 3538952 | tf_op jit(solution)/shard_map/ppermute | solution.py:26
  292.8 728.0 %all-gather.17.cloned.1.call-start = ((), (), s32[]{:S(2)}) async-start(), calls=%async_computation.7 | async-start | bytes 2181120 | tf_op jit(solution)/shard_map/all_gather | solution.py:116
  323.3 92.1 %collective-permute-start.7 = (bf16[2,192,2,1536]{3,2,1,0:T(2,128)(2,1)S(1)}, bf16[2,192,2,1536]{3,2,1,0:T(2,128)(2,1)S(1)}, u32[]{:S(2)}, u32[]{:S(2)}) collective-permute-start(bf16[2,192,2,1536]{3,2,1,0:T(2,128)(2,1)S(1)} %pad_maximum_fusion.15), channel_id=1, source_target_pairs={{0,8},{4,12},{8,0},{12,4},{16,24},{20,28},{24,16},{28,20},{1,9},{5... | collective-permute-start | bytes 7077896 | tf_op jit(solution)/shard_map/ppermute | solution.py:26
  347.9 177.8 %collective-permute-start.4 = (bf16[2,192,2,1536]{3,2,1,0:T(2,128)(2,1)S(1)}, bf16[2,192,2,1536]{3,2,1,0:T(2,128)(2,1)S(1)}, u32[]{:S(2)}, u32[]{:S(2)}) collective-permute-start(bf16[2,192,2,1536]{3,2,1,0:T(2,128)(2,1)S(1)} %pad_maximum_fusion.14), channel_id=1, source_target_pairs={{0,8},{4,12},{8,0},{12,4},{16,24},{20,28},{24,16},{28,20},{1,9},{5... | collective-permute-start | bytes 7077896 | tf_op jit(solution)/shard_map/ppermute | solution.py:26
  549.6 413.3 %collective-permute-start.8 = (bf16[4,192,2,1536]{3,2,1,0:T(2,128)(2,1)}, bf16[4,192,2,1536]{3,2,1,0:T(2,128)(2,1)}, u32[]{:S(2)}, u32[]{:S(2)}) collective-permute-start(bf16[4,192,2,1536]{3,2,1,0:T(2,128)(2,1)} %pad_maximum_fusion.6), channel_id=1, source_target_pairs={{0,16},{4,20},{8,24},{12,28},{16,0},{20,4},{24,8},{28,12},{1,17},{... | collective-permute-start | bytes 14155784 | tf_op jit(solution)/shard_map/ppermute | solution.py:26
  555.1 428.7 %copy-start.20 = (f32[256,384]{1,0:T(8,128)}, f32[256,384]{1,0:T(8,128)S(1)}, u32[]{:S(2)}) copy-start(f32[256,384]{1,0:T(8,128)S(1)} %fusion.188) | copy-start | bytes 1179652
  574.2 487.4 %collective-permute-start.5 = (bf16[4,192,2,1536]{3,2,1,0:T(2,128)(2,1)}, bf16[4,192,2,1536]{3,2,1,0:T(2,128)(2,1)}, u32[]{:S(2)}, u32[]{:S(2)}) collective-permute-start(bf16[4,192,2,1536]{3,2,1,0:T(2,128)(2,1)} %pad_maximum_fusion.5), channel_id=1, source_target_pairs={{0,16},{4,20},{8,24},{12,28},{16,0},{20,4},{24,8},{28,12},{1,17},{... | collective-permute-start | bytes 14155784 | tf_op jit(solution)/shard_map/ppermute | solution.py:26
  986.1 203.5 %reduce-scatter.10.cloned.1.call-start = ((), (), s32[]{:S(2)}) async-start(), calls=%async_computation.10 | async-start | bytes 4362240 | tf_op jit(solution)/shard_map/reduce_scatter | solution.py:128
  1037.7 162.2 %reduce-scatter.8.cloned.1.call-start = ((), (), s32[]{:S(2)}) async-start(), calls=%async_computation.8 | async-start | bytes 4362240 | tf_op jit(solution)/shard_map/reduce_scatter | solution.py:124
  1105.6 184.0 %all-gather.27.cloned.1.call-start = ((), (), s32[]{:S(2)}) async-start(), calls=%async_computation.15 | async-start | bytes 2654208 | tf_op jit(solution)/shard_map/all_gather | solution.py:141
  1108.8 19.5 collective-permute-start.9
  1130.8 50.6 %collective-permute-start.10 = (bf16[2,192,2,1152]{3,1,2,0:T(8,128)(2,1)S(1)}, bf16[2,192,2,1152]{3,1,2,0:T(8,128)(2,1)}, u32[]{:S(2)}, u32[]{:S(2)}) collective-permute-start(bf16[2,192,2,1152]{3,1,2,0:T(8,128)(2,1)S(1)} %pad_maximum_fusion.16), channel_id=1, source_target_pairs={{0,8},{4,12},{8,0},{12,4},{16,24},{20,28},{24,16},{28,20},{1,9},{5... | collective-permute-start | bytes 5308424 | tf_op jit(solution)/shard_map/ppermute | solution.py:26
  1134.5 241.1 %all-gather.21.cloned.1.call-start = ((), (), s32[]{:S(2)}) async-start(), calls=%async_computation.11 | async-start | bytes 2181120 | tf_op jit(solution)/shard_map/all_gather | solution.py:120
  1186.1 171.1 %collective-permute-start.11 = (bf16[4,192,2,1152]{3,1,2,0:T(8,128)(2,1)}, bf16[4,192,2,1152]{3,1,2,0:T(8,128)(2,1)}, u32[]{:S(2)}, u32[]{:S(2)}) collective-permute-start(bf16[4,192,2,1152]{3,1,2,0:T(8,128)(2,1)} %pad_maximum_fusion.7), channel_id=1, source_target_pairs={{0,16},{4,20},{8,24},{12,28},{16,0},{20,4},{24,8},{28,12},{1,17},{... | collective-permute-start | bytes 10616840 | tf_op jit(solution)/shard_map/ppermute | solution.py:26
  1206.6 457.2 %reduce-scatter.12.cloned.1.call-start = ((), (), s32[]{:S(2)}) async-start(), calls=%async_computation.12 | async-start | bytes 4362240 | tf_op jit(solution)/shard_map/reduce_scatter | solution.py:128
  1461.0 641.5 %all-reduce.13.cloned.1.call-start = ((), (), s32[]{:S(2)}) async-start(), calls=%async_computation.17 | async-start | bytes 37748736
  1533.7 1693.5 %all-reduce.15.cloned.1.call-start = ((), (), s32[]{:S(2)}) async-start(), calls=%async_computation.18 | async-start | bytes 75497472
  (79 other events, 1160.8 us)
Sparse Core Ops, SparseCore 0:
  11.9 94.9 all-reduce.10
  109.7 107.8 all-gather.14
  219.8 18.7 all-gather.12
  281.9 39.9 reduce-scatter.5
  323.3 20.5 all-gather.18
  346.5 193.6 all-gather.24
  542.3 383.3 all-gather.22
  986.2 19.4 all-gather.16
  1037.8 38.8 reduce-scatter.9
  1105.7 40.0 reduce-scatter.7
  1148.5 141.0 all-gather.26
  1291.6 20.9 all-gather.20
  1461.1 38.9 reduce-scatter.11
  1533.9 568.6 all-reduce.12
  2106.6 1120.5 all-reduce.14
